TPU v7x, 32 devices: a whole 2x2x4 slice. The times are simulated.
32 devices in a mesh: px: 2 (over x), py: 16 (over z, y, core).
Axes of the slice: x: 2, y: 2, z: 4, core: 2. Of those that a mesh axis runs over, the one named last changes fastest.
Arguments:
- populations: float32 [19, 2, 256, 512], P(None, None, ('py', 'px')), may hold values from 0.02 to 0.12
- pore: int32 [2, 256, 512], P(None, ('py', 'px')), may hold values 0 or 1
Outputs:
- flow: float32 [19, 2, 256, 512], P(None, None, 'py', 'px')
All inputs are finite; a program needn't handle non-finite values. No bound on the sum of `pore` on one device may be relied on, other than what follows from the above.
Results may differ from a plain program's by a relative error of at most 0.0001.
Values sent between devices are 32-bit elements; how exact they have to be, the bound alone decides.
A program may use at most 128 MiB of HBM per device.

v0:
```python
import jax
import jax.numpy as jnp
from jax import lax
from jax.sharding import PartitionSpec as P

STEPS = 2
lattice_velocity = [
    (0, 0, 0),
    (1, 0, 0),
    (-1, 0, 0),
    (0, 1, 0),
    (0, -1, 0),
    (0, 0, 1),
    (0, 0, -1),
    (1, 1, 0),
    (-1, -1, 0),
    (1, -1, 0),
    (-1, 1, 0),
    (1, 0, 1),
    (-1, 0, -1),
    (1, 0, -1),
    (-1, 0, 1),
    (0, 1, 1),
    (0, -1, -1),
    (0, 1, -1),
    (0, -1, 1),
]
lattice_weights = [1.0 / 3.0] + [1.0 / 18.0] * 6 + [1.0 / 36.0] * 12
opposite = [0, 2, 1, 4, 3, 6, 5, 8, 7, 10, 9, 12, 11, 14, 13, 16, 15, 18, 17]
relax_time = 0.8
body_force = 0.005


def with_halo(cells, sides, width):
    for axis, dim in sides:
        count = lax.axis_size(axis)
        head = lax.slice_in_dim(cells, 0, width, axis=dim)
        tail = lax.slice_in_dim(cells, cells.shape[dim] - width, cells.shape[dim], axis=dim)
        cells = jnp.concatenate(
            [
                lax.ppermute(tail, axis, [(i, (i + 1) % count) for i in range(count)]),
                cells,
                lax.ppermute(head, axis, [((i + 1) % count, i) for i in range(count)]),
            ],
            axis=dim,
        )
    return cells


def moment(fields, column):
    total = jnp.zeros_like(fields[0])
    for slot in range(len(lattice_velocity)):
        vector = lattice_velocity[slot]
        if vector[column] != 0:
            total = total + float(vector[column]) * fields[slot]
    return total


def collide(fields, fluid):
    density = jnp.where(fluid > 0.5, jnp.sum(fields, axis=0), 1.0)
    vel_first = moment(fields, 0) / density
    vel_second = moment(fields, 1) / density
    vel_third = moment(fields, 2) / density + relax_time * body_force
    speed = vel_first * vel_first + vel_second * vel_second + vel_third * vel_third
    result = []
    for slot in range(len(lattice_velocity)):
        vector = lattice_velocity[slot]
        along = vector[0] * vel_first + vector[1] * vel_second + vector[2] * vel_third
        equil = (
            lattice_weights[slot]
            * density
            * (1.0 + 3.0 * along + 4.5 * along * along - 1.5 * speed)
        )
        result.append(fields[slot] - (fields[slot] - equil) / relax_time)
    return jnp.stack(result) * fluid[None]


def stream(post, fluid):
    height = post.shape[2]
    width = post.shape[3]
    result = []
    for slot in range(len(lattice_velocity)):
        vector = lattice_velocity[slot]
        rows_from = 1 - vector[1]
        cols_from = 1 - vector[0]
        source = post[
            slot, :, rows_from : height - 2 + rows_from, cols_from : width - 2 + cols_from
        ]
        source = jnp.roll(source, vector[2], axis=0)
        open_cell = fluid[:, rows_from : height - 2 + rows_from, cols_from : width - 2 + cols_from]
        open_cell = jnp.roll(open_cell, vector[2], axis=0)
        bounced = post[opposite[slot], :, 1:-1, 1:-1]
        result.append(jnp.where(open_cell > 0.5, source, bounced))
    return jnp.stack(result) * fluid[None, :, 1:-1, 1:-1]


def body(populations, pore):
    count = populations.shape[0]
    stacked = jnp.concatenate([populations, pore.astype(jnp.float32)[None]], axis=0)
    pencil = lax.all_to_all(stacked, "px", split_axis=3, concat_axis=2, tiled=True)
    fields = pencil[:count]
    padded = with_halo(pencil, (("px", 3), ("py", 2)), 2)
    region = padded[count]
    fields = padded[:count]
    for step in range(STEPS):
        post = collide(fields, region)
        fields = stream(post, region)
        region = region[:, 1:-1, 1:-1]
    return fields


def solution(mesh):
    return jax.shard_map(
        body,
        mesh=mesh,
        in_specs=(P(None, None, ("py", "px"), None), P(None, ("py", "px"), None)),
        out_specs=P(None, None, "py", "px"),
        check_vma=False,
    )
```

profile of v0, /device:TPU:0, one launch (start us, length us, event | category | flops | bytes accessed | tf_op | source)
XLA Modules:
  0.0 70.4 jit_solution(6749811037562610711)
XLA Ops:
  0.0 0.8 %convert_bitcast_fusion = f32[1,2,8,512]{3,2,1,0:T(8,128)S(1)} fusion(s32[2,8,512]{2,1,0:T(8,128)} %param.3), kind=kLoop, calls=%fused_computation.539 | loop fusion | flops 8192 | bytes 65536 | tf_op jit(solution)/shard_map/broadcast_in_dim | solution.py:99
  0.8 1.1 %pad_maximum_fusion.1 = f32[20,2,8,512]{3,2,1,0:T(8,128)S(1)} fusion(f32[1,2,8,512]{3,2,1,0:T(8,128)S(1)} %convert_bitcast_fusion, f32[19,2,8,512]{3,2,1,0:T(8,128)} %param.2), kind=kLoop, calls=%fused_computation.5 | loop fusion | flops 163840 | bytes 1310720 | tf_op jit(solution)/shard_map/concatenate | solution.py:99
  1.9 3.8 %copy.6 = f32[20,2,8,512]{0,2,1,3:T(8,128)} copy(f32[20,2,8,512]{3,2,1,0:T(8,128)S(1)} %pad_maximum_fusion.1) | data formatting | bytes 1310720 | tf_op jit(solution)/shard_map/concatenate | solution.py:99
  5.7 6.0 %reshape.453 = f32[2,1,81920]{2,1,0:T(1,128)S(1)} reshape(f32[512,2,8,20]{3,2,1,0:T(8,128)} %bitcast.557) | data formatting | bytes 1310720
  11.7 13.4 %all_to_all.18 = f32[2,1,81920]{2,1,0:T(1,128)S(1)} all-to-all(f32[2,1,81920]{2,1,0:T(1,128)S(1)} %reshape.453), channel_id=1, replica_groups=mesh['px'=2,'py'=16] {'px'}, dimensions={0} | all-to-all | bytes 1310720 | tf_op jit(solution)/shard_map/all_to_all | solution.py:100
  25.1 0.5 broadcast.1003
  25.6 2.7 %reduce = f32[2,81920]{1,0:T(2,128)S(1)} reduce(f32[2,1,81920]{2,1,0:T(1,128)S(1)} %all_to_all.18, f32[]{:T(128)} %broadcast.1003), dimensions={1}, to_apply=%all_to_all.13.reduce_sub_computation | reduce | bytes 1310724 | tf_op jit(solution)/shard_map/all_to_all | solution.py:100
  28.4 6.9 %reshape.454 = f32[512,2,8,20]{3,2,1,0:T(8,128)} reshape(f32[2,81920]{1,0:T(2,128)S(1)} %reduce) | data formatting | bytes 1310720
  35.3 3.0 %copy.7 = f32[20,2,2,8,256]{4,3,2,1,0:T(8,128)S(1)} copy(f32[20,2,2,8,256]{0,3,1,4,2:T(8,128)} %bitcast.558) | data formatting | bytes 1310720 | tf_op jit(solution)/shard_map/all_to_all | solution.py:100
  38.3 0.2 fusion.285
  38.5 0.3 collective-permute-start
  38.8 1.7 %collective-permute-start.1 = (f32[20,2,16,2]{3,2,1,0:T(8,128)S(1)}, f32[20,2,16,2]{3,2,1,0:T(8,128)S(1)}, u32[]{:S(2)}, u32[]{:S(2)}) collective-permute-start(f32[20,2,16,2]{3,2,1,0:T(8,128)S(1)} %get-tuple-element.82), channel_id=1, source_target_pairs={{16,0},{0,16},{17,1},{1,17},{18,2},{2,18},{19,3},{3,19},{20,4},{4,... | collective-permute-start | bytes 15368 | tf_op jit(solution)/shard_map/ppermute | solution.py:43
  40.6 8.6 %collective-permute-done = f32[20,2,16,2]{3,2,1,0:T(8,128)S(1)} collective-permute-done((f32[20,2,16,2]{3,2,1,0:T(8,128)S(1)}, f32[20,2,16,2]{3,2,1,0:T(8,128)S(1)}, u32[]{:S(2)}, u32[]{:S(2)}) %collective-permute-start) | collective-permute-done | bytes 5152 | tf_op jit(solution)/shard_map/ppermute | solution.py:41
  49.1 4.8 %collective-permute-done.1 = f32[20,2,16,2]{3,2,1,0:T(8,128)S(1)} collective-permute-done((f32[20,2,16,2]{3,2,1,0:T(8,128)S(1)}, f32[20,2,16,2]{3,2,1,0:T(8,128)S(1)}, u32[]{:S(2)}, u32[]{:S(2)}) %collective-permute-start.1) | collective-permute-done | bytes 5152 | tf_op jit(solution)/shard_map/ppermute | solution.py:43
  53.9 0.4 pad_maximum_fusion.4
  54.4 4.4 %collective-permute-start.3 = (f32[20,2,2,260]{3,2,1,0:T(2,128)S(1)}, f32[20,2,2,260]{3,2,1,0:T(2,128)S(1)}, u32[]{:S(2)}, u32[]{:S(2)}) collective-permute-start(f32[20,2,2,260]{3,2,1,0:T(2,128)S(1)} %get-tuple-element.80), channel_id=1, source_target_pairs={{1,0},{2,1},{3,2},{4,3},{5,4},{6,5},{7,6},{8,7},{9,8},{10,9},{11,1... | collective-permute-start | bytes 249608 | tf_op jit(solution)/shard_map/ppermute | solution.py:43
  58.8 2.7 %collective-permute-done.2 = f32[20,2,2,260]{3,2,1,0:T(2,128)S(1)} collective-permute-done((f32[20,2,2,260]{3,2,1,0:T(2,128)S(1)}, f32[20,2,2,260]{3,2,1,0:T(2,128)S(1)}, u32[]{:S(2)}, u32[]{:S(2)}) %collective-permute-start.2) | collective-permute-done | bytes 83232 | tf_op jit(solution)/shard_map/ppermute | solution.py:41
  61.5 0.6 pad_maximum_fusion
  62.1 0.1 slice_reduce_fusion
  62.2 0.2 constant_dynamic-update-slice_fusion.18
  63.3 0.1 broadcast_multiply_fusion.2
  63.5 0.1 constant_dynamic-update-slice_fusion.37
  63.5 0.2 fusion.284
  63.8 0.1 slice_bitcast_fusion.37
  64.0 0.1 slice.1091
  64.1 0.1 constant_dynamic-update-slice_fusion.36
  64.2 0.1 constant_dynamic-update-slice_fusion.35
  64.3 0.1 constant_dynamic-update-slice_fusion.34
  64.4 0.1 constant_dynamic-update-slice_fusion.33
  64.6 0.1 constant_dynamic-update-slice_fusion.32
  64.7 0.1 constant_dynamic-update-slice_fusion.31
  64.8 0.1 constant_dynamic-update-slice_fusion.30
  64.9 0.1 constant_dynamic-update-slice_fusion.29
  65.0 0.1 constant_dynamic-update-slice_fusion.28
  65.1 0.1 constant_dynamic-update-slice_fusion.27
  65.2 0.1 constant_dynamic-update-slice_fusion.26
  65.3 0.1 constant_dynamic-update-slice_fusion.25
  65.4 0.1 constant_dynamic-update-slice_fusion.24
  65.5 0.1 constant_dynamic-update-slice_fusion.23
  65.6 0.1 constant_dynamic-update-slice_fusion.22
  65.7 0.1 constant_dynamic-update-slice_fusion.21
  65.8 0.1 constant_dynamic-update-slice_fusion.20
  65.9 0.1 constant_dynamic-update-slice_fusion.19
  66.0 0.1 fusion.282
  66.2 0.2 constant_dynamic-update-slice_fusion.56
  67.3 0.1 broadcast_multiply_fusion
  67.5 0.1 fusion.283
  67.6 0.1 slice_bitcast_fusion.63
  67.9 0.1 constant_dynamic-update-slice_fusion.74
  68.0 0.1 constant_dynamic-update-slice_fusion.73
  68.1 0.1 constant_dynamic-update-slice_fusion.72
  68.2 0.1 constant_dynamic-update-slice_fusion.71
  68.3 0.1 constant_dynamic-update-slice_fusion.70
  68.5 0.1 constant_dynamic-update-slice_fusion.68
  68.6 0.1 constant_dynamic-update-slice_fusion.67
  68.7 0.1 constant_dynamic-update-slice_fusion.66
  68.7 0.1 constant_dynamic-update-slice_fusion.65
  68.8 0.1 constant_dynamic-update-slice_fusion.64
  68.9 0.1 constant_dynamic-update-slice_fusion.63
  69.1 0.1 constant_dynamic-update-slice_fusion.61
  69.2 0.1 constant_dynamic-update-slice_fusion.60
  69.2 0.1 constant_dynamic-update-slice_fusion.59
  69.3 0.1 constant_dynamic-update-slice_fusion.58
  69.5 0.9 %broadcast_multiply_fusion.3 = f32[19,2,16,256]{3,2,1,0:T(8,128)} fusion(f32[19,2,16,256]{3,2,1,0:T(8,128)S(1)} %constant_dynamic-update-slice_fusion.57, f32[2,16,256]{2,1,0:T(8,128)S(1)} %slice.1176), kind=kLoop, calls=%fused_computation.6 | loop fusion | flops 155648 | bytes 1277952 | tf_op jit(solution)/shard_map/mul | solution.py:94
  (45 shorter events, 2.4 us)
Async XLA Ops:
  38.5 10.6 %collective-permute-start = (f32[20,2,16,2]{3,2,1,0:T(8,128)S(1)}, f32[20,2,16,2]{3,2,1,0:T(8,128)S(1)}, u32[]{:S(2)}, u32[]{:S(2)}) collective-permute-start(f32[20,2,16,2]{3,2,1,0:T(8,128)S(1)} %get-tuple-element.81), channel_id=1, source_target_pairs={{0,16},{16,0},{1,17},{17,1},{2,18},{18,2},{3,19},{19,3},{4,20},{20... | collective-permute-start | bytes 15368 | tf_op jit(solution)/shard_map/ppermute | solution.py:41
  38.8 15.1 %collective-permute-start.1 = (f32[20,2,16,2]{3,2,1,0:T(8,128)S(1)}, f32[20,2,16,2]{3,2,1,0:T(8,128)S(1)}, u32[]{:S(2)}, u32[]{:S(2)}) collective-permute-start(f32[20,2,16,2]{3,2,1,0:T(8,128)S(1)} %get-tuple-element.82), channel_id=1, source_target_pairs={{16,0},{0,16},{17,1},{1,17},{18,2},{2,18},{19,3},{3,19},{20,4},{4,... | collective-permute-start | bytes 15368 | tf_op jit(solution)/shard_map/ppermute | solution.py:43
  54.3 7.2 %collective-permute-start.2 = (f32[20,2,2,260]{3,2,1,0:T(2,128)S(1)}, f32[20,2,2,260]{3,2,1,0:T(2,128)S(1)}, u32[]{:S(2)}, u32[]{:S(2)}) collective-permute-start(f32[20,2,2,260]{3,2,1,0:T(2,128)S(1)} %get-tuple-element.79), channel_id=1, source_target_pairs={{0,1},{1,2},{2,3},{3,4},{4,5},{5,6},{6,7},{7,8},{8,9},{9,10},{10,1... | collective-permute-start | bytes 249608 | tf_op jit(solution)/shard_map/ppermute | solution.py:41
  54.4 7.1 %collective-permute-start.3 = (f32[20,2,2,260]{3,2,1,0:T(2,128)S(1)}, f32[20,2,2,260]{3,2,1,0:T(2,128)S(1)}, u32[]{:S(2)}, u32[]{:S(2)}) collective-permute-start(f32[20,2,2,260]{3,2,1,0:T(2,128)S(1)} %get-tuple-element.80), channel_id=1, source_target_pairs={{1,0},{2,1},{3,2},{4,3},{5,4},{6,5},{7,6},{8,7},{9,8},{10,9},{11,1... | collective-permute-start | bytes 249608 | tf_op jit(solution)/shard_map/ppermute | solution.py:43
where the time goes:
time: 70.6 us; the launch traced here: 70.4 us
  local copies, waits for them, and re-layouts  21.5 us (30%)
  waiting for transfers between devices  16 us (23%)
  blocking collectives  13.4 us (19%)
  other arithmetic  12.5 us (18%)
  starting transfers between devices  6.58 us (9%)
    all_to_all x1, blocking collectives, body(): lax.all_to_all(stacked, 'px', split_axis=3, concat_axis=2, tiled=True)  13.4 us
    unnamed x4, local copies, waits for them, and re-layouts  13.1 us
    ppermute x2, waiting for transfers between devices, with_halo(): lax.ppermute(tail, axis, [(i, (i + 1) % count) for i in range(count)])  11.2 us
    ppermute x2, starting transfers between devices, with_halo(): lax.ppermute(head, axis, [((i + 1) % count, i) for i in range(count)])  6.17 us
    unnamed x69, other arithmetic  5.24 us
    ppermute x2, waiting for transfers between devices, with_halo(): lax.ppermute(head, axis, [((i + 1) % count, i) for i in range(count)])  4.76 us
    concatenate x1, local copies, waits for them, and re-layouts, body(): jnp.concatenate([populations, pore.astype(jnp.float32)[None]], axis=0)  3.79 us
    all_to_all x2, local copies, waits for them, and re-layouts, body(): lax.all_to_all(stacked, 'px', split_axis=3, concat_axis=2, tiled=True)  3.53 us
  transfers between devices with their start and end apart: 4, of which 3 were waited for; matrix products, arithmetic and copies ran while one was open for 0% of the time, Pallas kernels for 0%

commit v1 on v0

--- a/solution.py
+++ b/solution.py
@@ -97,7 +97,10 @@
 def body(populations, pore):
     count = populations.shape[0]
     stacked = jnp.concatenate([populations, pore.astype(jnp.float32)[None]], axis=0)
-    pencil = lax.all_to_all(stacked, "px", split_axis=3, concat_axis=2, tiled=True)
+    pencil = jnp.concatenate(
+        lax.all_to_all(jnp.stack(jnp.split(stacked, lax.axis_size("px"), axis=3)), "px", 0, 0),
+        axis=2,
+    )
     fields = pencil[:count]
     padded = with_halo(pencil, (("px", 3), ("py", 2)), 2)
     region = padded[count]

time: 70.6 us -> 47.7 us (0.68)
  local copies, waits for them, and re-layouts: 21.5 us -> 1.31 us
  other arithmetic: 12.5 us -> 9.85 us
    unnamed x4 -> x2, local copies, waits for them, and re-layouts: 13.1 us -> 0.16 us
    concatenate x1 -> x0, local copies, waits for them, and re-layouts: 3.79 us -> none  [body(): jnp.concatenate([populations, pore.astype(jnp.float32)[None]], axis=0)]
    all_to_all x2 -> x0, local copies, waits for them, and re-layouts: 3.53 us -> none  [body(): lax.all_to_all(stacked, 'px', split_axis=3, concat_axis=2, tiled=True)]
    all_to_all x1 -> x0, other arithmetic: 2.72 us -> none  [body(): lax.all_to_all(stacked, 'px', split_axis=3, concat_axis=2, tiled=True)]
    another operation x0 -> x2, other arithmetic: none -> 1.15 us  [body(): jnp.stack(jnp.split(stacked, lax.axis_size('px'), axis=3))]
    concatenate x1 -> x0, other arithmetic: 1.13 us -> none  [body(): jnp.concatenate([populations, pore.astype(jnp.float32)[None]], axis=0)]
where the time goes in v1:
time: 47.7 us; the launch traced here: 47.5 us
  waiting for transfers between devices  16 us (34%)
  blocking collectives  13.4 us (28%)
  other arithmetic  9.85 us (21%)
  starting transfers between devices  6.58 us (14%)
  local copies, waits for them, and re-layouts  1.31 us (3%)
    all_to_all x1, blocking collectives, body(): lax.all_to_all(jnp.stack(jnp.split(stacked, lax.axis_size('px'), axis=3))...  13.4 us
    ppermute x2, waiting for transfers between devices, with_halo(): lax.ppermute(tail, axis, [(i, (i + 1) % count) for i in range(count)])  11.2 us
    ppermute x2, starting transfers between devices, with_halo(): lax.ppermute(head, axis, [((i + 1) % count, i) for i in range(count)])  6.17 us
    unnamed x69, other arithmetic  5.26 us
    ppermute x2, waiting for transfers between devices, with_halo(): lax.ppermute(head, axis, [((i + 1) % count, i) for i in range(count)])  4.76 us
    another operation x2, other arithmetic, body(): jnp.stack(jnp.split(stacked, lax.axis_size('px'), axis=3))  1.15 us
  transfers between devices with their start and end apart: 4, of which 3 were waited for; matrix products, arithmetic and copies ran while one was open for 0% of the time, Pallas kernels for 0%

profile of v1, /device:TPU:0, one launch (start us, length us, event | category | flops | bytes accessed | tf_op | source)
XLA Modules:
  0.0 47.5 jit_solution(12936284110617349869)
XLA Ops:
  0.0 0.8 %convert_bitcast_fusion = f32[1,2,8,512]{3,2,1,0:T(8,128)S(1)} fusion(s32[2,8,512]{2,1,0:T(8,128)} %param.3), kind=kLoop, calls=%fused_computation.546 | loop fusion | flops 8192 | bytes 65536 | tf_op jit(solution)/shard_map/broadcast_in_dim | solution.py:99
  0.8 1.1 %fusion.1 = (f32[1,20,2,8,256]{4,3,2,1,0:T(8,128)S(1)}, f32[1,20,2,8,256]{4,3,2,1,0:T(8,128)S(1)}) fusion(f32[19,2,8,512]{3,2,1,0:T(8,128)} %param.2, f32[1,2,8,512]{3,2,1,0:T(8,128)S(1)} %convert_bitcast_fusion), kind=kLoop, calls=%fused_computation.10 | loop fusion | flops 163840 | bytes 1310720 | tf_op jit(solution)/shard_map/stack | solution.py:101
  1.9 13.4 %all_to_all.5 = f32[2,20,2,8,256]{4,3,2,1,0:T(8,128)S(1)} all-to-all(f32[2,20,2,8,256]{4,3,2,1,0:T(8,128)S(1)} %pad_maximum_fusion.1), channel_id=1, replica_groups=mesh['px'=2,'py'=16] {'px'}, dimensions={0} | all-to-all | bytes 1310720 | tf_op jit(solution)/shard_map/all_to_all | solution.py:101
  15.3 0.1 copy_bitcast_fusion
  15.4 0.2 fusion.288
  15.6 0.3 collective-permute-start
  15.9 1.7 %collective-permute-start.1 = (f32[20,2,16,2]{3,2,1,0:T(8,128)S(1)}, f32[20,2,16,2]{3,2,1,0:T(8,128)S(1)}, u32[]{:S(2)}, u32[]{:S(2)}) collective-permute-start(f32[20,2,16,2]{3,2,1,0:T(8,128)S(1)} %get-tuple-element.82), channel_id=1, source_target_pairs={{16,0},{0,16},{17,1},{1,17},{18,2},{2,18},{19,3},{3,19},{20,4},{4,... | collective-permute-start | bytes 15368 | tf_op jit(solution)/shard_map/ppermute | solution.py:43
  17.7 8.6 %collective-permute-done = f32[20,2,16,2]{3,2,1,0:T(8,128)S(1)} collective-permute-done((f32[20,2,16,2]{3,2,1,0:T(8,128)S(1)}, f32[20,2,16,2]{3,2,1,0:T(8,128)S(1)}, u32[]{:S(2)}, u32[]{:S(2)}) %collective-permute-start) | collective-permute-done | bytes 5152 | tf_op jit(solution)/shard_map/ppermute | solution.py:41
  26.2 4.8 %collective-permute-done.1 = f32[20,2,16,2]{3,2,1,0:T(8,128)S(1)} collective-permute-done((f32[20,2,16,2]{3,2,1,0:T(8,128)S(1)}, f32[20,2,16,2]{3,2,1,0:T(8,128)S(1)}, u32[]{:S(2)}, u32[]{:S(2)}) %collective-permute-start.1) | collective-permute-done | bytes 5152 | tf_op jit(solution)/shard_map/ppermute | solution.py:43
  31.0 0.4 pad_maximum_fusion.5
  31.5 4.4 %collective-permute-start.3 = (f32[20,2,2,260]{3,2,1,0:T(2,128)S(1)}, f32[20,2,2,260]{3,2,1,0:T(2,128)S(1)}, u32[]{:S(2)}, u32[]{:S(2)}) collective-permute-start(f32[20,2,2,260]{3,2,1,0:T(2,128)S(1)} %get-tuple-element.80), channel_id=1, source_target_pairs={{1,0},{2,1},{3,2},{4,3},{5,4},{6,5},{7,6},{8,7},{9,8},{10,9},{11,1... | collective-permute-start | bytes 249608 | tf_op jit(solution)/shard_map/ppermute | solution.py:43
  35.9 2.7 %collective-permute-done.2 = f32[20,2,2,260]{3,2,1,0:T(2,128)S(1)} collective-permute-done((f32[20,2,2,260]{3,2,1,0:T(2,128)S(1)}, f32[20,2,2,260]{3,2,1,0:T(2,128)S(1)}, u32[]{:S(2)}, u32[]{:S(2)}) %collective-permute-start.2) | collective-permute-done | bytes 83232 | tf_op jit(solution)/shard_map/ppermute | solution.py:41
  38.6 0.6 %pad_maximum_fusion = f32[20,2,20,260]{3,2,1,0:T(8,128)S(1)} fusion(f32[20,2,2,260]{3,2,1,0:T(2,128)S(1)} %collective-permute-done.3, f32[20,2,16,2]{3,2,1,0:T(8,128)S(1)} %collective-permute-done.1, f32[20,2,16,256]{3,2,1,0:T(8,128)S(1)} %copy_bitcast_fusion, f32[20,2,16,2]{3,2,1,0:T(8,128)S(1)} %collective-permute-done, ...), kind=kLoop, calls=%fused_computation | loop fusion | flops 832000 | bytes 1664000 | tf_op jit(solution)/shard_map/concatenate | solution.py:39
  39.2 0.1 slice_reduce_fusion
  39.3 0.2 constant_dynamic-update-slice_fusion.18
  40.4 0.1 broadcast_multiply_fusion.2
  40.5 0.1 constant_dynamic-update-slice_fusion.37
  40.6 0.2 fusion.287
  40.9 0.1 slice_bitcast_fusion.37
  41.0 0.1 slice.1083
  41.1 0.1 slice.1091
  41.2 0.1 constant_dynamic-update-slice_fusion.36
  41.3 0.1 constant_dynamic-update-slice_fusion.35
  41.4 0.1 constant_dynamic-update-slice_fusion.34
  41.5 0.1 constant_dynamic-update-slice_fusion.33
  41.7 0.1 constant_dynamic-update-slice_fusion.32
  41.8 0.1 constant_dynamic-update-slice_fusion.31
  41.9 0.1 constant_dynamic-update-slice_fusion.30
  42.0 0.1 constant_dynamic-update-slice_fusion.29
  42.1 0.1 constant_dynamic-update-slice_fusion.28
  42.2 0.1 constant_dynamic-update-slice_fusion.27
  42.3 0.1 constant_dynamic-update-slice_fusion.26
  42.4 0.1 constant_dynamic-update-slice_fusion.25
  42.5 0.1 constant_dynamic-update-slice_fusion.24
  42.6 0.1 constant_dynamic-update-slice_fusion.23
  42.7 0.1 constant_dynamic-update-slice_fusion.22
  42.8 0.1 constant_dynamic-update-slice_fusion.21
  42.9 0.1 constant_dynamic-update-slice_fusion.20
  43.0 0.1 constant_dynamic-update-slice_fusion.19
  43.1 0.1 fusion.285
  43.3 0.2 constant_dynamic-update-slice_fusion.56
  44.4 0.1 broadcast_multiply_fusion
  44.5 0.1 constant_dynamic-update-slice_fusion.75
  44.6 0.1 fusion.286
  44.7 0.1 slice_bitcast_fusion.63
  45.0 0.1 constant_dynamic-update-slice_fusion.74
  45.1 0.1 constant_dynamic-update-slice_fusion.73
  45.2 0.1 constant_dynamic-update-slice_fusion.72
  45.3 0.1 constant_dynamic-update-slice_fusion.71
  45.4 0.1 constant_dynamic-update-slice_fusion.70
  45.5 0.1 constant_dynamic-update-slice_fusion.69
  45.6 0.1 constant_dynamic-update-slice_fusion.68
  45.7 0.1 constant_dynamic-update-slice_fusion.67
  45.8 0.1 constant_dynamic-update-slice_fusion.66
  45.8 0.1 constant_dynamic-update-slice_fusion.65
  46.0 0.1 constant_dynamic-update-slice_fusion.64
  46.0 0.1 constant_dynamic-update-slice_fusion.63
  46.1 0.1 constant_dynamic-update-slice_fusion.62
  46.2 0.1 constant_dynamic-update-slice_fusion.61
  46.3 0.1 constant_dynamic-update-slice_fusion.60
  46.4 0.1 constant_dynamic-update-slice_fusion.59
  46.4 0.1 constant_dynamic-update-slice_fusion.58
  46.5 0.1 constant_dynamic-update-slice_fusion.57
  46.6 0.9 %broadcast_multiply_fusion.3 = f32[19,2,16,256]{3,2,1,0:T(8,128)} fusion(f32[19,2,16,256]{3,2,1,0:T(8,128)S(1)} %constant_dynamic-update-slice_fusion.57, f32[2,16,256]{2,1,0:T(8,128)S(1)} %slice.1176), kind=kLoop, calls=%fused_computation.13 | loop fusion | flops 155648 | bytes 1277952 | tf_op jit(solution)/shard_map/mul | solution.py:94
  (41 shorter events, 2.1 us)
Async XLA Ops:
  15.6 10.6 %collective-permute-start = (f32[20,2,16,2]{3,2,1,0:T(8,128)S(1)}, f32[20,2,16,2]{3,2,1,0:T(8,128)S(1)}, u32[]{:S(2)}, u32[]{:S(2)}) collective-permute-start(f32[20,2,16,2]{3,2,1,0:T(8,128)S(1)} %get-tuple-element.81), channel_id=1, source_target_pairs={{0,16},{16,0},{1,17},{17,1},{2,18},{18,2},{3,19},{19,3},{4,20},{20... | collective-permute-start | bytes 15368 | tf_op jit(solution)/shard_map/ppermute | solution.py:41
  15.9 15.1 %collective-permute-start.1 = (f32[20,2,16,2]{3,2,1,0:T(8,128)S(1)}, f32[20,2,16,2]{3,2,1,0:T(8,128)S(1)}, u32[]{:S(2)}, u32[]{:S(2)}) collective-permute-start(f32[20,2,16,2]{3,2,1,0:T(8,128)S(1)} %get-tuple-element.82), channel_id=1, source_target_pairs={{16,0},{0,16},{17,1},{1,17},{18,2},{2,18},{19,3},{3,19},{20,4},{4,... | collective-permute-start | bytes 15368 | tf_op jit(solution)/shard_map/ppermute | solution.py:43
  31.4 7.2 %collective-permute-start.2 = (f32[20,2,2,260]{3,2,1,0:T(2,128)S(1)}, f32[20,2,2,260]{3,2,1,0:T(2,128)S(1)}, u32[]{:S(2)}, u32[]{:S(2)}) collective-permute-start(f32[20,2,2,260]{3,2,1,0:T(2,128)S(1)} %get-tuple-element.79), channel_id=1, source_target_pairs={{0,1},{1,2},{2,3},{3,4},{4,5},{5,6},{6,7},{7,8},{8,9},{9,10},{10,1... | collective-permute-start | bytes 249608 | tf_op jit(solution)/shard_map/ppermute | solution.py:41
  31.5 7.1 %collective-permute-start.3 = (f32[20,2,2,260]{3,2,1,0:T(2,128)S(1)}, f32[20,2,2,260]{3,2,1,0:T(2,128)S(1)}, u32[]{:S(2)}, u32[]{:S(2)}) collective-permute-start(f32[20,2,2,260]{3,2,1,0:T(2,128)S(1)} %get-tuple-element.80), channel_id=1, source_target_pairs={{1,0},{2,1},{3,2},{4,3},{5,4},{6,5},{7,6},{8,7},{9,8},{10,9},{11,1... | collective-permute-start | bytes 249608 | tf_op jit(solution)/shard_map/ppermute | solution.py:43
